TPU v7x, 32 devices: a whole 2x2x4 slice. The times are simulated.
32 devices in a mesh: groups: 2 (over y), seq: 4 (over x, core), qset: 4 (over z).
Axes of the slice: x: 2, y: 2, z: 4, core: 2. Of those that a mesh axis runs over, the one named last changes fastest.
Arguments:
- states: bfloat16 [8, 4, 128, 4096], P(('groups', 'qset'), 'seq'), parts along dimension 0, may hold values from -7 to 7
- enc_gain: bfloat16 [4096], replicated, may hold values from 0.25 to 1.75
- dec_states: bfloat16 [16, 64, 4096], P(('groups', 'qset')), parts along dimension 0, may hold values from -7 to 7
- dec_gain: bfloat16 [4096], replicated, may hold values from 0.25 to 1.75
- query_weight: bfloat16 [4096, 4096], P(None, 'seq'), may hold values from -0.375 to 0.375
- key_value_weight: bfloat16 [4096, 2, 4096], P(None, None, 'seq'), may hold values from -0.0625 to 0.0625
- out_weight: bfloat16 [4096, 4096], P('seq'), may hold values from -0.75 to 0.75
- question_of: int32 [8, 4, 1], P('groups'), parts along dimension 0, may hold values from 0 to 7; in each aligned block of 4 rows (0 to 3, 4 to 7, ..., all dimensions but the last counted through in order) at most 2 rows name the same one
Outputs:
- mixed: bfloat16 [16, 64, 4096], P(('groups', 'qset'), None, 'seq'), parts along dimension 0
There are 2 independent parts, one for each index of `groups`. A program takes and returns all parts, laid end to end along the dimension named above; an argument that names none is the same for every part. Nothing has to cross between parts.
Inputs may be any that keep to these rules, and one draw needn't show every extreme that they name: `question_of`: within each index of the first dimension (one source group of 4 passages) at most 2 passages name the same question, and exactly 2 do for some question in some groups; every question is named by at least one passage.
All inputs are finite; a program needn't handle non-finite values.
Results may differ from a plain program's by a relative error of at most 0.014.
The roundings to bfloat16 on the way count: a program that leaves them out, or rounds other values in their place, can miss the bound.
Values may be sent and summed in bfloat16 or wider, within the bound.
A program may use at most 128 MiB of HBM per device.

v0:
```python
import jax
import jax.numpy as jnp
from jax import lax
from jax.sharding import PartitionSpec as P

HD = 64
CAP = 2


EPSILON = 1e-06
MASKED_SCORE = -1e30


def scaled_norm(rows_in, gain_vec):
    rows_f32 = rows_in.astype(jnp.float32)
    mean_square = jnp.mean(rows_f32 * rows_f32, axis=-1, keepdims=True)
    return rows_f32 * lax.rsqrt(mean_square + EPSILON) * gain_vec.astype(jnp.float32)


def body(
    states, enc_gain, dec_states, dec_gain, query_weight, key_value_weight, out_weight, question_of
):
    model_width = states.shape[-1]
    passage_len = states.shape[2]
    group_count = lax.axis_size("qset")
    shard_count = lax.axis_size("seq")
    group_index = lax.axis_index("qset")
    shard_index = lax.axis_index("seq")
    local_questions = dec_states.shape[0]
    dec_len = dec_states.shape[1]
    head_cols = query_weight.shape[1]
    heads_here = head_cols // HD
    all_questions = local_questions * group_count
    kv_weight = key_value_weight.reshape(model_width, 2 * head_cols)
    own_rows = scaled_norm(states[0, 0], enc_gain).astype(jnp.bfloat16)[None]
    gathered_rows = lax.all_gather(own_rows, "seq", axis=0, tiled=True)
    piece_count = gathered_rows.shape[0]
    flat_rows = gathered_rows.reshape(piece_count * passage_len, model_width)
    product = jnp.dot(flat_rows, kv_weight, preferred_element_type=jnp.float32)
    key_vals = product.astype(jnp.bfloat16).reshape(piece_count, passage_len, 2 * head_cols)
    passage_table = question_of[:, :, 0]
    numbers = jnp.arange(all_questions, dtype=jnp.int32)
    counts = jnp.sum(
        (passage_table[:, :, None] == numbers[None, None, :]).astype(jnp.int32), axis=1
    )
    group_table = lax.dynamic_index_in_dim(passage_table, group_index, 0, keepdims=False)
    matches = (group_table[:, None] == numbers[None, :]).astype(jnp.int32)
    earlier = jnp.cumsum(matches, axis=0) - matches
    slot_rank = jnp.sum(earlier * matches, axis=1)
    slot_index = group_table * CAP + slot_rank
    picker = (
        jnp.arange(all_questions * CAP, dtype=jnp.int32)[:, None] == slot_index[None, :]
    ).astype(jnp.bfloat16)
    packed = jnp.einsum("as,spc->apc", picker, key_vals, preferred_element_type=jnp.float32).astype(
        jnp.bfloat16
    )
    dec_rows = (
        scaled_norm(dec_states, dec_gain)
        .astype(jnp.bfloat16)
        .reshape(local_questions * dec_len, model_width)
    )
    queries = jnp.dot(dec_rows, query_weight, preferred_element_type=jnp.float32)
    queries = queries.astype(jnp.bfloat16).reshape(local_questions, dec_len, heads_here, HD)
    slot_numbers = jnp.arange(CAP, dtype=jnp.int32)
    gathered = lax.all_gather(queries, "qset", axis=0, tiled=True)
    local_keys = packed.reshape(all_questions, CAP * passage_len, 2 * head_cols)
    key_rows = local_keys[:, :, :head_cols].reshape(all_questions, -1, heads_here, HD)
    value_rows = local_keys[:, :, head_cols:].reshape(all_questions, -1, heads_here, HD)
    own_counts = lax.dynamic_index_in_dim(counts, group_index, 0, keepdims=False)
    live_slots = own_counts[:, None] > slot_numbers[None, :]
    live_rows = jnp.broadcast_to(live_slots[:, :, None], (all_questions, CAP, passage_len)).reshape(
        all_questions, -1
    )
    scores = jnp.einsum("qthd,qrhd->qhtr", gathered, key_rows, preferred_element_type=jnp.float32)
    scores = jnp.where(live_rows[:, None, None, :], scores, MASKED_SCORE)
    row_peak = lax.pmax(jnp.max(scores, axis=-1), "qset")
    weights = jnp.where(live_rows[:, None, None, :], jnp.exp(scores - row_peak[..., None]), 0.0)
    group_total = jnp.sum(weights, axis=-1)
    group_summed = jnp.einsum(
        "qhtr,qrhd->qthd",
        weights.astype(jnp.bfloat16),
        value_rows,
        preferred_element_type=jnp.float32,
    )
    summed, row_total = (
        lax.psum_scatter(
            group_summed.astype(jnp.bfloat16), "qset", scatter_dimension=0, tiled=True
        ).astype(jnp.float32),
        lax.psum_scatter(
            group_total.astype(jnp.bfloat16), "qset", scatter_dimension=0, tiled=True
        ).astype(jnp.float32),
    )
    attended = summed / jnp.transpose(row_total, (0, 2, 1))[..., None]
    attended = attended.astype(jnp.bfloat16).reshape(local_questions * dec_len, head_cols)
    piece_cols = model_width // shard_count
    residual = lax.dynamic_slice_in_dim(dec_states, shard_index * piece_cols, piece_cols, 2).astype(
        jnp.float32
    )
    full_sum = lax.psum(
        jnp.dot(attended, out_weight, preferred_element_type=jnp.float32).astype(jnp.bfloat16),
        "seq",
    ).astype(jnp.float32)
    owned_sum = lax.dynamic_slice_in_dim(full_sum, shard_index * piece_cols, piece_cols, 1)
    owned_sum = owned_sum.reshape(local_questions, dec_len, piece_cols)
    return (residual + owned_sum).astype(jnp.bfloat16)


def solution(mesh):
    return jax.shard_map(
        body,
        mesh=mesh,
        in_specs=(
            P(("groups", "qset"), "seq", None, None),
            P(),
            P(("groups", "qset"), None, None),
            P(),
            P(None, "seq"),
            P(None, None, "seq"),
            P("seq", None),
            P("groups", None, None),
        ),
        out_specs=P(("groups", "qset"), None, "seq"),
        check_vma=False,
    )
```

profile of v0, /device:TPU:0, one launch (start us, length us, event | category | flops | bytes accessed | tf_op | source)
XLA Modules:
  0.0 243.0 jit_solution(42193561007402769)
XLA Ops:
  6.5 0.8 convert_element_type.90
  7.3 1.5 fusion.14
  8.9 2.6 %fusion.13 = bf16[1,128,4096]{2,1,0:T(8,128)(2,1)} fusion(bf16[1,1,128,4096]{3,2,1,0:T(8,128)(2,1)} %param.8, f32[4096]{0:T(1024)S(1)} %convert_element_type.90, f32[128]{0:T(128)S(1)} %add_rsqrt_fusion.1), kind=kLoop, calls=%fused_computation.21 | loop fusion | flops 2097152 | bytes 2114048 | tf_op jit(solution)/shard_map/convert_element_type | solution.py:35
  12.2 4.7 %convolution_convert_fusion.3 = bf16[128,1024]{1,0:T(8,128)(2,1)S(1)} fusion(bf16[128,4096]{1,0:T(8,128)(2,1)S(1)} %bitcast.47, bf16[4096,1024]{1,0:T(8,128)(2,1)} %param.12), kind=kOutput, calls=%fused_computation.27 | convolution fusion | flops 1073872896 | bytes 9699328 | tf_op jit(solution)/shard_map/dot_general | solution.py:62
  16.9 1.1 reshape.157
  18.3 17.3 %copy.29 = bf16[512,8,2,1024]{3,1,2,0:T(8,128)(2,1)} copy(bf16[512,8,2,1024]{3,2,1,0:T(2,128)(2,1)} %bitcast.44) | data formatting | bytes 33554432
  36.1 12.7 %all-gather.3.cloned.1.call-done = bf16[4,128,4096]{2,1,0:T(8,128)(2,1)} async-done(((bf16[1,128,4096]{2,1,0:T(8,128)(2,1)}), bf16[4,128,4096]{2,1,0:T(8,128)(2,1)}) %all-gather.3.cloned.1.call-update) | async-done | bytes 4194320 | tf_op jit(solution)/shard_map/all_gather | solution.py:36
  48.8 13.6 %convolution_convert_fusion.2 = bf16[512,2048]{1,0:T(8,128)(2,1)S(1)} fusion(bf16[512,4096]{1,0:T(8,128)(2,1)} %bitcast.52, bf16[4096,2048]{1,0:T(8,128)(2,1)} %bitcast.45), kind=kOutput, calls=%fused_computation.11 | convolution fusion | flops 8590983168 | bytes 23068672 | tf_op jit(solution)/shard_map/dot_general | solution.py:39
  62.4 5.7 %convolution_convert_fusion = bf16[16,128,2048]{2,0,1:T(8,128)(2,1)} fusion(bf16[4,128,2048]{2,1,0:T(8,128)(2,1)S(1)} %bitcast.50, s32[4]{0:T(128)S(1)} %multiply_add_fusion), kind=kOutput, calls=%fused_computation.4 | convolution fusion | flops 37748800 | bytes 10485776 | tf_op jit(solution)/shard_map/as,spc->apc/dot_general | solution.py:54
  68.1 11.3 %copy.24 = bf16[16,128,2048]{2,1,0:T(8,128)(2,1)} copy(bf16[16,128,2048]{2,0,1:T(8,128)(2,1)} %convolution_convert_fusion) | data formatting | bytes 16777216 | tf_op jit(solution)/shard_map/convert_element_type | solution.py:54
  79.4 6.0 %fusion.28 = (bf16[8,256,1024]{2,1,0:T(8,128)(2,1)}, bf16[8,256,1024]{2,1,0:T(8,128)(2,1)}) fusion(bf16[8,256,2048]{2,1,0:T(8,128)(2,1)} %bitcast.43), kind=kLoop, calls=%fused_computation.51 | loop fusion | bytes 16777216 | tf_op jit(solution)/shard_map/slice | solution.py:67
  85.4 6.5 %copy.25 = bf16[8,256,1024]{1,2,0:T(8,128)(2,1)} copy(bf16[8,256,1024]{2,1,0:T(8,128)(2,1)} %get-tuple-element.6) | data formatting | bytes 8388608 | tf_op jit(solution)/shard_map/slice | solution.py:68
  91.8 6.4 %copy.26 = bf16[8,256,1024]{1,2,0:T(8,128)(2,1)} copy(bf16[8,256,1024]{2,1,0:T(8,128)(2,1)} %get-tuple-element.5) | data formatting | bytes 8388608 | tf_op jit(solution)/shard_map/slice | solution.py:67
  98.3 7.4 %select_reduce_fusion = (f32[8,16,64]{2,1,0:T(8,128)S(1)}, f32[8,16,64,256]{3,2,1,0:T(8,128)}) fusion(pred[8,256]{1,0:T(8,128)(4,1)S(1)} %broadcast_bitcast_fusion, bf16[8,256,16,64]{1,3,2,0:T(8,128)(2,1)} %bitcast.46, bf16[8,64,16,64]{3,2,1,0:T(8,128)(2,1)} %all-gather.5.cloned.1.call-done), kind=kOutput, calls=%fused_computation.1 | convolution fusion | flops 272621568 | bytes 13666304 | tf_op jit(solution)/shard_map/qthd,qrhd->qhtr/dot_general | solution.py:74
  105.6 19.6 %pmax.7 = f32[8,16,64]{2,1,0:T(8,128)S(1)} all-reduce(f32[8,16,64]{2,1,0:T(8,128)S(1)} %get-tuple-element.7), channel_id=1, replica_groups=mesh['groups'=2,'seq'=4,'qset'=4] {'qset'}, use_global_device_ids=true, to_apply=%region_6.7 | all-reduce | flops 8192 | bytes 65536 | tf_op jit(solution)/shard_map/pmax | solution.py:76
  125.2 5.4 %fusion = bf16[8,16,64]{2,1,0:T(8,128)(2,1)} fusion(f32[8,16,64,256]{3,2,1,0:T(8,128)} %get-tuple-element.8, f32[8,16,64]{2,1,0:T(8,128)S(1)} %pmax.7, pred[8,256]{1,0:T(8,128)(4,1)S(1)} %broadcast_bitcast_fusion), kind=kLoop, calls=%fused_computation.2 | loop fusion | flops 8380416 | bytes 8439808 | tf_op jit(solution)/shard_map/reduce_sum | solution.py:78
  130.7 7.7 %convert_bitcast_fusion.1 = bf16[8,64,16,64]{1,3,2,0:T(8,128)(2,1)} fusion(bf16[8,256,16,64]{1,3,2,0:T(8,128)(2,1)} %bitcast.48, f32[8,16,64,256]{3,2,1,0:T(8,128)} %get-tuple-element.8, f32[8,16,64]{2,1,0:T(8,128)S(1)} %pmax.7, pred[8,256]{1,0:T(8,128)(4,1)S(1)} %broadcast_bitcast_fusion), kind=kOutput, calls=%fused_computation.26 | convolution fusion | flops 277348352 | bytes 13666304 | tf_op jit(solution)/shard_map/qhtr,qrhd->qthd/dot_general | solution.py:79
  138.5 8.8 %reduce-scatter.5.cloned.1.call-done = bf16[2,16,64]{2,1,0:T(8,128)(2,1)} async-done(((bf16[8,16,64]{2,1,0:T(8,128)(2,1)}), bf16[2,16,64]{2,1,0:T(8,128)(2,1)}) %reduce-scatter.5.cloned.1.call-update) | async-done | bytes 4112 | tf_op jit(solution)/shard_map/reduce_scatter | solution.py:89
  148.0 43.3 %reduce-scatter.3.cloned.1.call-done = bf16[2,64,16,64]{1,3,2,0:T(8,128)(2,1)} async-done(((bf16[8,64,16,64]{1,3,2,0:T(8,128)(2,1)}), bf16[2,64,16,64]{1,3,2,0:T(8,128)(2,1)}) %reduce-scatter.3.cloned.1.call-update) | async-done | bytes 262160 | tf_op jit(solution)/shard_map/reduce_scatter | solution.py:86
  191.3 1.2 divide_convert_fusion
  193.3 5.7 %convolution_convert_fusion.1 = bf16[128,4096]{1,0:T(8,128)(2,1)} fusion(bf16[128,1024]{1,0:T(8,128)(2,1)S(1)} %reshape.159, bf16[1024,4096]{1,0:T(8,128)(2,1)} %param.14), kind=kOutput, calls=%fused_computation.5 | convolution fusion | flops 1074266112 | bytes 9699328 | tf_op jit(solution)/shard_map/dot_general | solution.py:100
  199.0 35.6 %all-reduce.2.cloned.1.call-done = bf16[128,4096]{1,0:T(8,128)(2,1)} async-done(((bf16[128,4096]{1,0:T(8,128)(2,1)}), bf16[128,4096]{1,0:T(8,128)(2,1)}) %all-reduce.2.cloned.1.call-update) | async-done | bytes 1048592 | tf_op jit(solution)/shard_map/psum | solution.py:99
  234.7 1.0 dynamic-slice_convert_fusion
  235.7 0.8 add_convert_fusion
  (34 shorter events, 3.1 us)
Async XLA Ops:
  6.5 5.0 %copy-start.1 = (bf16[4096]{0:T(1024)(128)(2,1)S(1)}, bf16[4096]{0:T(1024)(128)(2,1)}, u32[]{:S(2)}) copy-start(bf16[4096]{0:T(1024)(128)(2,1)} %param.11) | copy-start | bytes 24580
  6.5 5.0 %copy-start = (bf16[2,64,4096]{2,1,0:T(8,128)(2,1)S(1)}, bf16[2,64,4096]{2,1,0:T(8,128)(2,1)}, u32[]{:S(2)}) copy-start(bf16[2,64,4096]{2,1,0:T(8,128)(2,1)} %param.10) | copy-start | bytes 3145732
  6.5 42.2 %all-gather.3.cloned.1.call-start = ((), (), s32[]{:S(2)}) async-start(), calls=%async_computation.2 | async-start | bytes 5242880 | tf_op jit(solution)/shard_map/all_gather | solution.py:36
  11.4 86.8 %all-gather.5.cloned.1.call-start = ((), (), s32[]{:S(2)}) async-start(), calls=%async_computation.3 | async-start | bytes 2621440 | tf_op jit(solution)/shard_map/all_gather | solution.py:65
  18.0 129.3 %reduce-scatter.5.cloned.1.call-start = ((), (), s32[]{:S(2)}) async-start(), calls=%async_computation.5 | async-start | bytes 40960 | tf_op jit(solution)/shard_map/reduce_scatter | solution.py:89
  18.3 17.3 %copy-start.2 = (s32[4,4,1]{1,2,0:T(1,128)S(1)}, s32[4,4,1]{1,2,0:T(1,128)}, u32[]{:S(2)}) copy-start(s32[4,4,1]{1,2,0:T(1,128)} %param.15) | copy-start | bytes 196
  130.7 60.7 %reduce-scatter.3.cloned.1.call-start = ((), (), s32[]{:S(2)}) async-start(), calls=%async_computation.4 | async-start | bytes 2621440 | tf_op jit(solution)/shard_map/reduce_scatter | solution.py:86
  138.5 96.2 %all-reduce.2.cloned.1.call-start = ((), (), s32[]{:S(2)}) async-start(), calls=%async_computation.6 | async-start | bytes 2097152 | tf_op jit(solution)/shard_map/psum | solution.py:99
Sparse Core Ops, SparseCore 0:
  11.6 37.1 all-gather.2
  50.3 45.6 all-gather.4
  130.8 16.4 reduce-scatter.4
  149.5 41.8 reduce-scatter.2
  199.2 35.4 all-reduce.1
where the time goes:
time: 244 us; the launch traced here: 243 us
  waiting for transfers between devices  101 us (41%)
  local copies, waits for them, and re-layouts  49.5 us (20%)
  matrix products  44.7 us (18%)
  blocking collectives  19.6 us (8%)
  other arithmetic  15 us (6%)
  between operations  13.3 us (5%)
    reduce_scatter x1, waiting for transfers between devices, body(): lax.psum_scatter(group_summed.astype(jnp.bfloat16), 'qset', scatter_dimen...  43.3 us
    psum x1, waiting for transfers between devices, body(): lax.psum(jnp.dot(attended, out_weight, preferred_element_type=jnp.float32...  35.6 us
    pmax x1, blocking collectives, body(): row_peak = lax.pmax(jnp.max(scores, axis=-1), 'qset')  19.6 us
    unnamed x7, local copies, waits for them, and re-layouts  17.3 us
    dot_general x1, matrix products, body(): product = jnp.dot(flat_rows, kv_weight, preferred_element_type=jnp.float32)  13.6 us
    all_gather x1, waiting for transfers between devices, body(): gathered_rows = lax.all_gather(own_rows, 'seq', axis=0, tiled=True)  12.7 us
    slice x2, local copies, waits for them, and re-layouts, body(): local_keys[:, :, :head_cols].reshape(all_questions, -1, heads_here, HD)  12.5 us
    convert_element_type x1, local copies, waits for them, and re-layouts, body(): jnp.einsum('as,spc->apc', picker, key_vals, preferred_element_type=jnp.fl...  11.3 us
  transfers between devices with their start and end apart: 5, of which 4 were waited for; matrix products, arithmetic and copies ran while one was open for 34% of the time, Pallas kernels for 0%

commit v1 on v0

v1 whole, which is shorter than its diff:
```python
import functools
import jax
import jax.numpy as jnp
from jax import lax
from jax.experimental import pallas as pl
from jax.experimental.pallas import tpu as pltpu
from jax.sharding import PartitionSpec as P

HD = 64
EPSILON = 1e-06
DEAD = -1e30
CHUNKS = 4
F32 = jnp.float32
BF16 = jnp.bfloat16


def norm_rows(load, store, gain, rows):
    step = 16

    def one(i, carry):
        at = pl.ds(pl.multiple_of(i * step, step), step)
        x = load(at).astype(F32)
        ms = jnp.mean(x * x, axis=-1, keepdims=True)
        store(at, (x * lax.rsqrt(ms + EPSILON) * gain).astype(BF16))
        return carry

    lax.fori_loop(0, rows // step, one, 0)


def kernel(
    cfg, qo, states, enc_gain, dec_states, dec_gain, qw, kvw, ow, out,
    gat, qw_v, kv_v, ow_v, xn, kvs, qall, a_s, e_s, psend, ssend, precv, srecv,
    att, rsend, rpart, rx, rown,
    local_sem, xs_send, xs_recv, q_send, q_recv, p_send, p_recv, s_send, s_recv,
    d_send, d_recv, r_send, r_recv,
):
    n_seq, nz, nlq, plen, dlen, width, cols = cfg
    nx = n_seq // 2
    npairs = cols // 128
    rows = nlq * dlen
    me = lax.axis_index("seq")
    z = lax.axis_index("qset")
    x = me // 2
    c = lax.rem(me, 2)
    partner = x * 2 + (1 - c)

    def seq_of(dx, core):
        return lax.rem(x + dx, nx) * 2 + core

    own_copy = pltpu.make_async_copy(states, gat.at[me], local_sem.at[0])
    own_copy.start()
    qw_copy = pltpu.make_async_copy(qw, qw_v, local_sem.at[1])
    qw_copy.start()
    kv_copy = pltpu.make_async_copy(kvw, kv_v, local_sem.at[2])
    kv_copy.start()
    ow_copy = pltpu.make_async_copy(ow, ow_v, local_sem.at[3])

    barrier = pltpu.get_barrier_semaphore()
    for dx in range(1, nx):
        pl.semaphore_signal(barrier, 1, device_id={"seq": seq_of(dx, c)})
    pl.semaphore_signal(barrier, 1, device_id={"seq": partner})
    for dz in range(1, nz):
        pl.semaphore_signal(barrier, 1, device_id={"qset": lax.rem(z + dz, nz)})
    pl.semaphore_wait(barrier, nx - 1 + 1 + nz - 1)

    own_copy.wait()
    crows = plen // CHUNKS

    def state_copy(slot, ch, to, send_sem):
        part = gat.at[slot, pl.ds(ch * crows, crows)]
        return pltpu.make_async_remote_copy(
            src_ref=part, dst_ref=part, send_sem=send_sem,
            recv_sem=xs_recv.at[slot, ch], device_id={"seq": to},
        )

    pending = []
    for ch in range(CHUNKS):
        for dx in range(1, nx):
            cp = state_copy(me, ch, seq_of(dx, c), xs_send.at[0, dx, ch])
            cp.start()
            pending.append(cp)
        cp = state_copy(me, ch, partner, xs_send.at[0, 0, ch])
        cp.start()
        pending.append(cp)

    dg = dec_gain[...].astype(F32)
    eg = enc_gain[...].astype(F32)

    def put_xn(base):
        def put(at, v):
            xn[pl.ds(pl.multiple_of(base + at.start, 16), at.size), :] = v
        return put

    norm_rows(lambda at: dec_states[at, :], put_xn(0), dg, rows)
    qw_copy.wait()
    ow_copy.start()
    tile = min(256, cols)

    def q_tile(i, carry):
        at = pl.ds(pl.multiple_of(i * tile, tile), tile)
        r = jnp.dot(xn[:rows, :], qw_v[:, at], preferred_element_type=F32).astype(BF16)
        for lq in range(nlq):
            qall[z * nlq + lq, :, at] = r[lq * dlen:(lq + 1) * dlen]
        return carry

    lax.fori_loop(0, cols // tile, q_tile, 0)
    own_q = qall.at[pl.ds(z * nlq, nlq)]
    for dz in range(1, nz):
        cp = pltpu.make_async_remote_copy(
            src_ref=own_q, dst_ref=own_q, send_sem=q_send.at[dz],
            recv_sem=q_recv.at[z], device_id={"qset": lax.rem(z + dz, nz)},
        )
        cp.start()
        pending.append(cp)

    def wait_slot(slot, ch):
        state_copy(slot, ch, partner, xs_send.at[0, 0, 0]).wait_recv()

    def project(xi):
        for k in range(2):
            norm_rows(lambda at: gat[xi * 2 + k, at, :], put_xn(k * plen), eg, plen)

        def kv_tile(i, carry):
            at = pl.ds(pl.multiple_of(i * tile, tile), tile)
            kvs[xi, :, at] = jnp.dot(
                xn[...], kv_v[:, at], preferred_element_type=F32
            ).astype(BF16)
            return carry

        lax.fori_loop(0, 2 * cols // tile, kv_tile, 0)

    for ch in range(CHUNKS):
        wait_slot(partner, ch)
    kv_copy.wait()
    project(x)
    for dx in range(1, nx):
        for ch in range(CHUNKS):
            slot = seq_of(dx, c)
            wait_slot(slot, ch)
            cp = state_copy(slot, ch, partner, xs_send.at[1, dx, ch])
            cp.start()
            pending.append(cp)
    for dx in range(1, nx):
        for ch in range(CHUNKS):
            wait_slot(seq_of(dx, 1 - c), ch)
        project(lax.rem(x + dx, nx))

    for dz in range(1, nz):
        zs = lax.rem(z + dz, nz)
        src = qall.at[pl.ds(zs * nlq, nlq)]
        pltpu.make_async_remote_copy(
            src_ref=src, dst_ref=src, send_sem=q_send.at[0],
            recv_sem=q_recv.at[zs], device_id={"qset": zs},
        ).wait_recv()

    low = lax.broadcasted_iota(jnp.int32, (dlen, 128), 1) < HD
    lane = lax.broadcasted_iota(jnp.int32, (dlen, 128), 1)

    def attend(p, carry):
        qp = qall[qo[z, p]]
        xi = p // 2
        at = pl.ds(pl.multiple_of(lax.rem(p, 2) * plen, plen), plen)
        for j in range(npairs):
            q = qp[:, j * 128:(j + 1) * 128]
            zero = jnp.zeros_like(q)
            q2 = jnp.concatenate([jnp.where(low, q, zero), jnp.where(low, zero, q)], axis=0)
            k = kvs[xi, at, pl.ds(j * 128, 128)]
            v = kvs[xi, at, pl.ds(cols + j * 128, 128)]
            s = lax.dot_general(q2, k, (((1,), (1,)), ((), ())), preferred_element_type=F32)
            m = jnp.max(s, axis=-1, keepdims=True)
            w = jnp.exp(s - m)
            l = jnp.sum(w, axis=-1, keepdims=True)
            o = jnp.dot(w.astype(BF16), v, preferred_element_type=F32) / l
            e = jnp.broadcast_to(m + jnp.log(l), o.shape)
            a_s[p, :, pl.ds(j * 128, 128)] = jnp.where(low, o[:dlen], o[dlen:])
            e_s[p, :, pl.ds(j * 128, 128)] = jnp.where(low, e[:dlen], e[dlen:])
        return carry

    lax.fori_loop(0, n_seq, attend, 0)

    for dz in list(range(1, nz)) + [0]:
        dest = lax.rem(z + dz, nz)
        packed = jnp.zeros((dlen, 128), F32)
        for lq in range(nlq):
            question = dest * nlq + lq
            first = jnp.int32(0)
            second = jnp.int32(0)
            count = jnp.int32(0)
            for p in range(n_seq):
                hit = qo[z, p] == question
                first = jnp.where(hit & (count == 0), p, first)
                second = jnp.where(hit & (count == 1), p, second)
                count = count + hit.astype(jnp.int32)
            for j in range(npairs):
                at = pl.ds(j * 128, 128)
                e1 = jnp.where(count >= 1, e_s[first, :, at], DEAD)
                e2 = jnp.where(count >= 2, e_s[second, :, at], DEAD)
                top = jnp.maximum(e1, e2)
                w1 = jnp.exp(e1 - top)
                w2 = jnp.exp(e2 - top)
                tot = w1 + w2
                a = (w1 * a_s[first, :, at] + w2 * a_s[second, :, at]) / tot
                a = jnp.where(count >= 1, a, 0.0).astype(BF16)
                le = jnp.where(count >= 1, top + jnp.log(tot), DEAD)
                packed = jnp.where((lane & (HD - 1)) == lq * npairs + j, le, packed)
                if dz == 0:
                    precv[z, pl.ds(lq * dlen, dlen), at] = a
                else:
                    psend[dz, pl.ds(lq * dlen, dlen), at] = a
        if dz == 0:
            srecv[z] = packed
        else:
            ssend[dz] = packed
            for src, dst, ss, rs in (
                (ssend, srecv, s_send, s_recv), (psend, precv, p_send, p_recv),
            ):
                cp = pltpu.make_async_remote_copy(
                    src_ref=src.at[dz], dst_ref=dst.at[z], send_sem=ss.at[dz],
                    recv_sem=rs.at[z], device_id={"qset": dest},
                )
                cp.start()
                pending.append(cp)
    for dz in range(1, nz):
        zs = lax.rem(z + dz, nz)
        for src, dst, ss, rs in (
            (ssend, srecv, s_send, s_recv), (psend, precv, p_send, p_recv),
        ):
            pltpu.make_async_remote_copy(
                src_ref=src.at[dz], dst_ref=dst.at[zs], send_sem=ss.at[0],
                recv_sem=rs.at[zs], device_id={"qset": zs},
            ).wait_recv()
    for lq in range(nlq):
        for j in range(npairs):
            at = pl.ds(j * 128, 128)
            i = lq * npairs + j
            es = []
            for zs in range(nz):
                t = srecv[zs]
                es.append(jnp.where(low, t[:, i:i + 1], t[:, HD + i:HD + i + 1]))
            top = functools.reduce(jnp.maximum, es)
            tot = jnp.zeros((dlen, 128), F32)
            acc = jnp.zeros((dlen, 128), F32)
            for zs in range(nz):
                w = jnp.exp(es[zs] - top)
                tot = tot + w
                acc = acc + w * precv[zs, pl.ds(lq * dlen, dlen), at].astype(F32)
            att[pl.ds(lq * dlen, dlen), at] = (acc / tot).astype(BF16)

    ow_copy.wait()
    piece = width // n_seq
    ptile = min(256, piece)

    def project_out(dest, put):
        def one(i, carry):
            src = pl.ds(pl.multiple_of(dest * piece + i * ptile, 128), ptile)
            at = pl.ds(pl.multiple_of(i * ptile, ptile), ptile)
            put(at, src, jnp.dot(att[...], ow_v[:, src], preferred_element_type=F32))
            return carry

        lax.fori_loop(0, piece // ptile, one, 0)

    order = list(range(1, nx)) + [0]
    for dx in order:
        def put_send(at, src, r):
            rsend[dx, :, at] = r.astype(BF16)

        project_out(seq_of(dx, 1 - c), put_send)
        cp = pltpu.make_async_remote_copy(
            src_ref=rsend.at[dx], dst_ref=rpart.at[dx], send_sem=d_send.at[dx],
            recv_sem=d_recv.at[dx], device_id={"seq": partner},
        )
        cp.start()
        pending.append(cp)

    def wait_part(dx):
        pltpu.make_async_remote_copy(
            src_ref=rsend.at[dx], dst_ref=rpart.at[dx], send_sem=d_send.at[dx],
            recv_sem=d_recv.at[dx], device_id={"seq": partner},
        ).wait_recv()

    for dx in order:
        def put_sum(at, src, r):
            rown[:, at] = r

        project_out(seq_of(dx, c), put_sum)
        wait_part(dx)
        if dx:
            rsend[nx + dx] = (rown[...] + rpart[dx].astype(F32)).astype(BF16)
            cp = pltpu.make_async_remote_copy(
                src_ref=rsend.at[nx + dx], dst_ref=rx.at[x], send_sem=r_send.at[dx],
                recv_sem=r_recv.at[x], device_id={"seq": seq_of(dx, c)},
            )
            cp.start()
            pending.append(cp)
        else:
            mine = pl.ds(pl.multiple_of(me * piece, 128), piece)
            rown[...] = rown[...] + rpart[0].astype(F32) + dec_states[:, mine].astype(F32)
    total = rown[...]
    for dx in range(1, nx):
        xs = lax.rem(x + dx, nx)
        pltpu.make_async_remote_copy(
            src_ref=rsend.at[0], dst_ref=rx.at[xs], send_sem=r_send.at[0],
            recv_sem=r_recv.at[xs], device_id={"seq": xs * 2 + c},
        ).wait_recv()
        total = total + rx[xs].astype(F32)
    out[...] = total.astype(BF16)
    for cp in pending:
        cp.wait_send()


def body(
    states, enc_gain, dec_states, dec_gain, query_weight, key_value_weight, out_weight, question_of
):
    nz = lax.axis_size("qset")
    n_seq = lax.axis_size("seq")
    nx = n_seq // 2
    plen, width = states.shape[2], states.shape[3]
    nlq, dlen = dec_states.shape[0], dec_states.shape[1]
    cols = query_weight.shape[1]
    rows = nlq * dlen
    piece = width // n_seq
    cfg = (n_seq, nz, nlq, plen, dlen, width, cols)
    any_spec = pl.BlockSpec(memory_space=pl.ANY)
    vmem = pl.BlockSpec(memory_space=pltpu.VMEM)
    dma = pltpu.SemaphoreType.DMA
    result = pl.pallas_call(
        functools.partial(kernel, cfg),
        out_shape=jax.ShapeDtypeStruct((rows, piece), BF16),
        in_specs=[pl.BlockSpec(memory_space=pltpu.SMEM), any_spec, vmem, vmem, vmem,
                  any_spec, any_spec, any_spec],
        out_specs=vmem,
        scratch_shapes=[
            pltpu.VMEM((n_seq, plen, width), BF16),
            pltpu.VMEM((width, cols), BF16),
            pltpu.VMEM((width, 2 * cols), BF16),
            pltpu.VMEM((cols, width), BF16),
            pltpu.VMEM((2 * plen, width), BF16),
            pltpu.VMEM((nx, 2 * plen, 2 * cols), BF16),
            pltpu.VMEM((nlq * nz, dlen, cols), BF16),
            pltpu.VMEM((n_seq, dlen, cols), F32),
            pltpu.VMEM((n_seq, dlen, cols), F32),
            pltpu.VMEM((nz, rows, cols), BF16),
            pltpu.VMEM((nz, dlen, 128), F32),
            pltpu.VMEM((nz, rows, cols), BF16),
            pltpu.VMEM((nz, dlen, 128), F32),
            pltpu.VMEM((rows, cols), BF16),
            pltpu.VMEM((2 * nx, rows, piece), BF16),
            pltpu.VMEM((nx, rows, piece), BF16),
            pltpu.VMEM((nx, rows, piece), BF16),
            pltpu.VMEM((rows, piece), F32),
            dma((4,)),
            dma((2, nx, CHUNKS)), dma((n_seq, CHUNKS)),
            dma((nz,)), dma((nz,)), dma((nz,)), dma((nz,)), dma((nz,)), dma((nz,)),
            dma((nx,)), dma((nx,)), dma((nx,)), dma((nx,)),
        ],
        compiler_params=pltpu.CompilerParams(
            collective_id=0, has_side_effects=True, vmem_limit_bytes=63 * 1024 * 1024
        ),
        name="reader",
    )(
        question_of[:, :, 0], states.reshape(plen, width), enc_gain.reshape(1, width),
        dec_states.reshape(rows, width), dec_gain.reshape(1, width),
        query_weight, key_value_weight.reshape(width, 2 * cols), out_weight,
    )
    return result.reshape(nlq, dlen, piece)


def solution(mesh):
    return jax.shard_map(
        body,
        mesh=mesh,
        in_specs=(
            P(("groups", "qset"), "seq", None, None),
            P(),
            P(("groups", "qset"), None, None),
            P(),
            P(None, "seq"),
            P(None, None, "seq"),
            P("seq", None),
            P("groups", None, None),
        ),
        out_specs=P(("groups", "qset"), None, "seq"),
        check_vma=False,
    )
```

time: 244 us -> 108 us (0.44)
  the two profiles are of different devices: /device:TPU:0 before, /device:TPU:11 now
where the time goes in v1:
time: 108 us; the launch traced here: 107 us
  Pallas kernels  85.9 us (80%)
  local copies, waits for them, and re-layouts  21.4 us (20%)
    pallas_call x1, Pallas kernels, body(): pl.pallas_call(functools.partial(kernel, cfg), out_shape=jax.ShapeDtypeSt...  85.9 us
    unnamed x2, local copies, waits for them, and re-layouts  18.8 us

profile of v1, /device:TPU:11, one launch (start us, length us, event | category | flops | bytes accessed | tf_op | source)
XLA Modules:
  0.0 107.3 jit_solution(9590653474989173901)
XLA Ops:
  0.0 1.3 %reshape.19.enc_gain = bf16[1,4096]{1,0:T(2,128)(2,1)} reshape(bf16[4096]{0:T(1024)(128)(2,1)} %param.9) | data formatting | bytes 16384 | tf_op jit(solution)/shard_map/reshape | solution.py:361
  1.3 1.3 %reshape.21.dec_gain = bf16[1,4096]{1,0:T(2,128)(2,1)} reshape(bf16[4096]{0:T(1024)(128)(2,1)} %param.11) | data formatting | bytes 16384 | tf_op jit(solution)/shard_map/reshape | solution.py:362
  2.6 17.1 %copy.9 = bf16[512,8,2,1024]{3,1,2,0:T(8,128)(2,1)} copy(bf16[512,8,2,1024]{3,2,1,0:T(2,128)(2,1)} %bitcast.7) | data formatting | bytes 33554432
  19.7 85.9 %reader.1 = bf16[128,1024]{1,0:T(8,128)(2,1)} custom-call(s32[4,4]{1,0:T(4,128)} %bitcast.11, bf16[128,4096]{1,0:T(8,128)(2,1)} %bitcast.9, bf16[1,4096]{1,0:T(2,128)(2,1)} %reshape.19.enc_gain, bf16[128,4096]{1,0:T(8,128)(2,1)} %bitcast.10, bf16[1,4096]{1,0:T(2,128)(2,1)} %reshape.21.dec_gain, bf16[4096,1024]{1,0:T(8,128)(2,1)} %qw.1, ...), custom_call_target="tpu_custom_call" | custom-call | tf_op jit(solution)/shard_map/reader/pallas_call | solution.py:326
  105.6 1.7 %copy.11 = bf16[2,64,1024]{2,1,0:T(8,128)(2,1)} copy(bf16[2,64,1024]{2,1,0:T(8,128)(2,1)} %bitcast.8) | data formatting | bytes 524288

commit v2 on v1

--- a/solution.py
+++ b/solution.py
@@ -29,15 +29,18 @@
 
 def kernel(
     cfg, qo, states, enc_gain, dec_states, dec_gain, qw, kvw, ow, out,
-    gat, qw_v, kv_v, ow_v, xn, kvs, qall, a_s, e_s, psend, ssend, precv, srecv,
-    att, rsend, rpart, rx, rown,
-    local_sem, xs_send, xs_recv, q_send, q_recv, p_send, p_recv, s_send, s_recv,
+    gat, qw_v, raw, pulled, kv_v, ow_v, xn, kvs, qall, a_s, e_s, psend, ssend, precv, srecv,
+    att, oacc, rsend, rpart, rx, rown,
+    local_sem, raw_sem, xs_send, xs_recv, q_send, q_recv, p_send, p_recv, s_send, s_recv,
     d_send, d_recv, r_send, r_recv,
 ):
     n_seq, nz, nlq, plen, dlen, width, cols = cfg
     nx = n_seq // 2
     npairs = cols // 128
     rows = nlq * dlen
+    nch = 4 if npairs % 4 == 0 else npairs
+    pc = npairs // nch
+    cw = pc * 128
     me = lax.axis_index("seq")
     z = lax.axis_index("qset")
     x = me // 2
@@ -51,8 +54,16 @@
     own_copy.start()
     qw_copy = pltpu.make_async_copy(qw, qw_v, local_sem.at[1])
     qw_copy.start()
-    kv_copy = pltpu.make_async_copy(kvw, kv_v, local_sem.at[2])
-    kv_copy.start()
+    nblocks = cols // 128
+    slots = raw.shape[0]
+
+    def raw_copy(b):
+        return pltpu.make_async_copy(
+            kvw.at[:, :, pl.ds(b * 128, 128)], raw.at[b % slots], raw_sem.at[b % slots]
+        )
+
+    for b in range(min(slots, nblocks)):
+        raw_copy(b).start()
     ow_copy = pltpu.make_async_copy(ow, ow_v, local_sem.at[3])
 
     barrier = pltpu.get_barrier_semaphore()
@@ -83,8 +94,8 @@
         cp.start()
         pending.append(cp)
 
-    dg = dec_gain[...].astype(F32)
-    eg = enc_gain[...].astype(F32)
+    dg = dec_gain[...].astype(F32).reshape(1, width)
+    eg = enc_gain[...].astype(F32).reshape(1, width)
 
     def put_xn(base):
         def put(at, v):
@@ -116,34 +127,65 @@
     def wait_slot(slot, ch):
         state_copy(slot, ch, partner, xs_send.at[0, 0, 0]).wait_recv()
 
-    def project(xi):
+    def project(xi, start, count):
         for k in range(2):
-            norm_rows(lambda at: gat[xi * 2 + k, at, :], put_xn(k * plen), eg, plen)
+            norm_rows(
+                lambda at: gat[xi * 2 + k, pl.ds(pl.multiple_of(start + at.start, 16), at.size), :],
+                put_xn(k * count), eg, count,
+            )
 
         def kv_tile(i, carry):
             at = pl.ds(pl.multiple_of(i * tile, tile), tile)
-            kvs[xi, :, at] = jnp.dot(
-                xn[...], kv_v[:, at], preferred_element_type=F32
+            r = jnp.dot(
+                xn[:2 * count, :], kv_v[:, at], preferred_element_type=F32
             ).astype(BF16)
+            for k in range(2):
+                kvs[xi, pl.ds(k * plen + start, count), at] = r[k * count:(k + 1) * count]
             return carry
 
         lax.fori_loop(0, 2 * cols // tile, kv_tile, 0)
 
-    for ch in range(CHUNKS):
-        wait_slot(partner, ch)
-    kv_copy.wait()
-    project(x)
-    for dx in range(1, nx):
-        for ch in range(CHUNKS):
+    def forward(ch):
+        for dx in range(1, nx):
             slot = seq_of(dx, c)
             wait_slot(slot, ch)
             cp = state_copy(slot, ch, partner, xs_send.at[1, dx, ch])
             cp.start()
             pending.append(cp)
+
+    half = pulled.shape[0] // 2
+    for b in range(nblocks):
+        raw_copy(b).wait()
+        flat = raw.at[b % slots].reshape(2 * width, 128)
+
+        def pull(i, carry):
+            pulled[...] = flat[pl.ds(pl.multiple_of(i * 2 * half, 2 * half), 2 * half), :].astype(F32)
+            at = pl.ds(pl.multiple_of(i * half, half), half)
+            kv_v[at, pl.ds(b * 128, 128)] = pulled[pl.ds(0, half, stride=2), :].astype(BF16)
+            kv_v[at, pl.ds(cols + b * 128, 128)] = pulled[pl.ds(1, half, stride=2), :].astype(BF16)
+            return carry
+
+        lax.fori_loop(0, width // half, pull, 0)
+        if b + slots < nblocks:
+            raw_copy(b + slots).start()
+        if b == nblocks // 2:
+            forward(0)
+
+    for ch in range(CHUNKS):
+        wait_slot(partner, ch)
+    forward(1)
+    project(x, 0, plen)
+    forward(2)
+    part = plen // 2
     for dx in range(1, nx):
-        for ch in range(CHUNKS):
+        for ch in range(CHUNKS // 2):
             wait_slot(seq_of(dx, 1 - c), ch)
-        project(lax.rem(x + dx, nx))
+        project(lax.rem(x + dx, nx), 0, part)
+    forward(3)
+    for dx in range(1, nx):
+        for ch in range(CHUNKS // 2, CHUNKS):
+            wait_slot(seq_of(dx, 1 - c), ch)
+        project(lax.rem(x + dx, nx), part, part)
 
     for dz in range(1, nz):
         zs = lax.rem(z + dz, nz)
@@ -156,12 +198,15 @@
     low = lax.broadcasted_iota(jnp.int32, (dlen, 128), 1) < HD
     lane = lax.broadcasted_iota(jnp.int32, (dlen, 128), 1)
 
-    def attend(p, carry):
-        qp = qall[qo[z, p]]
+    groups = dlen // 8
+
+    def attend(g, p):
+        qp = qall[qo[z, p], :, pl.ds(g * cw, cw)]
         xi = p // 2
         at = pl.ds(pl.multiple_of(lax.rem(p, 2) * plen, plen), plen)
-        for j in range(npairs):
-            q = qp[:, j * 128:(j + 1) * 128]
+        for i in range(pc):
+            j = g * pc + i
+            q = qp[:, i * 128:(i + 1) * 128]
             zero = jnp.zeros_like(q)
             q2 = jnp.concatenate([jnp.where(low, q, zero), jnp.where(low, zero, q)], axis=0)
             k = kvs[xi, at, pl.ds(j * 128, 128)]
@@ -172,81 +217,99 @@
             l = jnp.sum(w, axis=-1, keepdims=True)
             o = jnp.dot(w.astype(BF16), v, preferred_element_type=F32) / l
             e = jnp.broadcast_to(m + jnp.log(l), o.shape)
-            a_s[p, :, pl.ds(j * 128, 128)] = jnp.where(low, o[:dlen], o[dlen:])
-            e_s[p, :, pl.ds(j * 128, 128)] = jnp.where(low, e[:dlen], e[dlen:])
-        return carry
-
-    lax.fori_loop(0, n_seq, attend, 0)
-
-    for dz in list(range(1, nz)) + [0]:
-        dest = lax.rem(z + dz, nz)
-        packed = jnp.zeros((dlen, 128), F32)
-        for lq in range(nlq):
-            question = dest * nlq + lq
-            first = jnp.int32(0)
-            second = jnp.int32(0)
-            count = jnp.int32(0)
-            for p in range(n_seq):
-                hit = qo[z, p] == question
-                first = jnp.where(hit & (count == 0), p, first)
-                second = jnp.where(hit & (count == 1), p, second)
-                count = count + hit.astype(jnp.int32)
-            for j in range(npairs):
-                at = pl.ds(j * 128, 128)
-                e1 = jnp.where(count >= 1, e_s[first, :, at], DEAD)
-                e2 = jnp.where(count >= 2, e_s[second, :, at], DEAD)
-                top = jnp.maximum(e1, e2)
-                w1 = jnp.exp(e1 - top)
-                w2 = jnp.exp(e2 - top)
-                tot = w1 + w2
-                a = (w1 * a_s[first, :, at] + w2 * a_s[second, :, at]) / tot
-                a = jnp.where(count >= 1, a, 0.0).astype(BF16)
-                le = jnp.where(count >= 1, top + jnp.log(tot), DEAD)
-                packed = jnp.where((lane & (HD - 1)) == lq * npairs + j, le, packed)
-                if dz == 0:
-                    precv[z, pl.ds(lq * dlen, dlen), at] = a
-                else:
-                    psend[dz, pl.ds(lq * dlen, dlen), at] = a
-        if dz == 0:
-            srecv[z] = packed
-        else:
-            ssend[dz] = packed
+            a_s[p, :, pl.ds(i * 128, 128)] = jnp.where(low, o[:dlen], o[dlen:])
+            e_s[p, :, pl.ds(i * 128, 128)] = jnp.where(low, e[:dlen], e[dlen:])
+
+    def exchange(g, dz, sender):
+        zs = lax.rem(z + dz, nz)
+        to = z if sender else zs
+        return [
+            pltpu.make_async_remote_copy(
+                src_ref=src.at[g, dz], dst_ref=dst.at[g, to], send_sem=ss.at[g, dz],
+                recv_sem=rs.at[g, to], device_id={"qset": zs},
+            )
             for src, dst, ss, rs in (
                 (ssend, srecv, s_send, s_recv), (psend, precv, p_send, p_recv),
-            ):
-                cp = pltpu.make_async_remote_copy(
-                    src_ref=src.at[dz], dst_ref=dst.at[z], send_sem=ss.at[dz],
-                    recv_sem=rs.at[z], device_id={"qset": dest},
+            )
+        ]
+
+    for g in range(nch):
+        lax.fori_loop(0, n_seq, lambda p, carry: (attend(g, p), carry)[1], 0, unroll=4)
+        for dz in list(range(1, nz)) + [0]:
+            dest = lax.rem(z + dz, nz)
+            packed = jnp.zeros((dlen, 128), F32)
+            for lq in range(nlq):
+                question = dest * nlq + lq
+                first = jnp.int32(0)
+                second = jnp.int32(0)
+                count = jnp.int32(0)
+                for p in range(n_seq):
+                    hit = qo[z, p] == question
+                    first = jnp.where(hit & (count == 0), p, first)
+                    second = jnp.where(hit & (count == 1), p, second)
+                    count = count + hit.astype(jnp.int32)
+                for i in range(pc):
+                    at = pl.ds(i * 128, 128)
+                    e1 = jnp.where(count >= 1, e_s[first, :, at], DEAD)
+                    e2 = jnp.where(count >= 2, e_s[second, :, at], DEAD)
+                    top = jnp.maximum(e1, e2)
+                    w1 = jnp.exp(e1 - top)
+                    w2 = jnp.exp(e2 - top)
+                    tot = w1 + w2
+                    a = (w1 * a_s[first, :, at] + w2 * a_s[second, :, at]) / tot
+                    a = jnp.where(count >= 1, a, 0.0).astype(BF16)
+                    le = jnp.where(count >= 1, top + jnp.log(tot), DEAD)
+                    packed = jnp.where((lane & (HD - 1)) == lq * pc + i, le, packed)
+                    if dz == 0:
+                        precv[g, z, pl.ds(lq * dlen, dlen), at] = a
+                    else:
+                        psend[g, dz, pl.ds(lq * dlen, dlen), at] = a
+            tight = jnp.zeros((8, 128), F32)
+            for t in range(groups):
+                piece8 = packed[t * 8:(t + 1) * 8]
+                tight = tight + (pltpu.roll(piece8, t * 8, 1) if t else piece8)
+            if dz == 0:
+                srecv[g, z] = tight
+            else:
+                ssend[g, dz] = tight
+                for cp in exchange(g, dz, True):
+                    cp.start()
+                    pending.append(cp)
+    ow_copy.wait()
+    otile = min(256, width // n_seq)
+    for g in range(nch):
+        for dz in range(1, nz):
+            for cp in exchange(g, dz, False):
+                cp.wait_recv()
+        spread = []
+        for zs in range(nz):
+            t8 = srecv[g, zs]
+            spread.append(jnp.concatenate(
+                [pltpu.roll(t8, 128 - t * 8, 1) if t else t8 for t in range(groups)], axis=0))
+        for lq in range(nlq):
+            for i in range(pc):
+                at = pl.ds(i * 128, 128)
+                n = lq * pc + i
+                es = [jnp.where(low, t[:, n:n + 1], t[:, HD + n:HD + n + 1]) for t in spread]
+                top = functools.reduce(jnp.maximum, es)
+                tot = jnp.zeros((dlen, 128), F32)
+                acc = jnp.zeros((dlen, 128), F32)
+                for zs in range(nz):
+                    w = jnp.exp(es[zs] - top)
+                    tot = tot + w
+                    acc = acc + w * precv[g, zs, pl.ds(lq * dlen, dlen), at].astype(F32)
+                att[g, pl.ds(lq * dlen, dlen), at] = (acc / tot).astype(BF16)
+        if g < nch - 1:
+            def early(i, carry):
+                at = pl.ds(pl.multiple_of(i * otile, otile), otile)
+                r = jnp.dot(
+                    att[g], ow_v[pl.ds(g * cw, cw), at], preferred_element_type=F32
                 )
-                cp.start()
-                pending.append(cp)
-    for dz in range(1, nz):
-        zs = lax.rem(z + dz, nz)
-        for src, dst, ss, rs in (
-            (ssend, srecv, s_send, s_recv), (psend, precv, p_send, p_recv),
-        ):
-            pltpu.make_async_remote_copy(
-                src_ref=src.at[dz], dst_ref=dst.at[zs], send_sem=ss.at[0],
-                recv_sem=rs.at[zs], device_id={"qset": zs},
-            ).wait_recv()
-    for lq in range(nlq):
-        for j in range(npairs):
-            at = pl.ds(j * 128, 128)
-            i = lq * npairs + j
-            es = []
-            for zs in range(nz):
-                t = srecv[zs]
-                es.append(jnp.where(low, t[:, i:i + 1], t[:, HD + i:HD + i + 1]))
-            top = functools.reduce(jnp.maximum, es)
-            tot = jnp.zeros((dlen, 128), F32)
-            acc = jnp.zeros((dlen, 128), F32)
-            for zs in range(nz):
-                w = jnp.exp(es[zs] - top)
-                tot = tot + w
-                acc = acc + w * precv[zs, pl.ds(lq * dlen, dlen), at].astype(F32)
-            att[pl.ds(lq * dlen, dlen), at] = (acc / tot).astype(BF16)
-
-    ow_copy.wait()
+                oacc[:, at] = r if g == 0 else oacc[:, at] + r
+                return carry
+
+            lax.fori_loop(0, width // otile, early, 0)
+
     piece = width // n_seq
     ptile = min(256, piece)
 
@@ -254,7 +317,10 @@
         def one(i, carry):
             src = pl.ds(pl.multiple_of(dest * piece + i * ptile, 128), ptile)
             at = pl.ds(pl.multiple_of(i * ptile, ptile), ptile)
-            put(at, src, jnp.dot(att[...], ow_v[:, src], preferred_element_type=F32))
+            r = jnp.dot(
+                att[nch - 1], ow_v[pl.ds((nch - 1) * cw, cw), src], preferred_element_type=F32
+            )
+            put(at, src, oacc[:, src] + r if nch > 1 else r)
             return carry
 
         lax.fori_loop(0, piece // ptile, one, 0)
@@ -319,6 +385,9 @@
     cols = query_weight.shape[1]
     rows = nlq * dlen
     piece = width // n_seq
+    npairs = cols // 128
+    nch = 4 if npairs % 4 == 0 else npairs
+    cw = cols // nch
     cfg = (n_seq, nz, nlq, plen, dlen, width, cols)
     any_spec = pl.BlockSpec(memory_space=pl.ANY)
     vmem = pl.BlockSpec(memory_space=pltpu.VMEM)
@@ -332,25 +401,29 @@
         scratch_shapes=[
             pltpu.VMEM((n_seq, plen, width), BF16),
             pltpu.VMEM((width, cols), BF16),
+            pltpu.VMEM((2, width, 2, 128), BF16),
+            pltpu.VMEM((1024, 128), F32),
             pltpu.VMEM((width, 2 * cols), BF16),
             pltpu.VMEM((cols, width), BF16),
             pltpu.VMEM((2 * plen, width), BF16),
             pltpu.VMEM((nx, 2 * plen, 2 * cols), BF16),
             pltpu.VMEM((nlq * nz, dlen, cols), BF16),
-            pltpu.VMEM((n_seq, dlen, cols), F32),
-            pltpu.VMEM((n_seq, dlen, cols), F32),
-            pltpu.VMEM((nz, rows, cols), BF16),
-            pltpu.VMEM((nz, dlen, 128), F32),
-            pltpu.VMEM((nz, rows, cols), BF16),
-            pltpu.VMEM((nz, dlen, 128), F32),
-            pltpu.VMEM((rows, cols), BF16),
+            pltpu.VMEM((n_seq, dlen, cw), F32),
+            pltpu.VMEM((n_seq, dlen, cw), F32),
+            pltpu.VMEM((nch, nz, rows, cw), BF16),
+            pltpu.VMEM((nch, nz, 8, 128), F32),
+            pltpu.VMEM((nch, nz, rows, cw), BF16),
+            pltpu.VMEM((nch, nz, 8, 128), F32),
+            pltpu.VMEM((nch, rows, cw), BF16),
+            pltpu.VMEM((rows, width), F32),
             pltpu.VMEM((2 * nx, rows, piece), BF16),
             pltpu.VMEM((nx, rows, piece), BF16),
             pltpu.VMEM((nx, rows, piece), BF16),
             pltpu.VMEM((rows, piece), F32),
-            dma((4,)),
+            dma((4,)), dma((2,)),
             dma((2, nx, CHUNKS)), dma((n_seq, CHUNKS)),
-            dma((nz,)), dma((nz,)), dma((nz,)), dma((nz,)), dma((nz,)), dma((nz,)),
+            dma((nz,)), dma((nz,)),
+            dma((nch, nz)), dma((nch, nz)), dma((nch, nz)), dma((nch, nz)),
             dma((nx,)), dma((nx,)), dma((nx,)), dma((nx,)),
         ],
         compiler_params=pltpu.CompilerParams(
@@ -358,9 +431,9 @@
         ),
         name="reader",
     )(
-        question_of[:, :, 0], states.reshape(plen, width), enc_gain.reshape(1, width),
-        dec_states.reshape(rows, width), dec_gain.reshape(1, width),
-        query_weight, key_value_weight.reshape(width, 2 * cols), out_weight,
+        question_of[:, :, 0], states.reshape(plen, width), enc_gain,
+        dec_states.reshape(rows, width), dec_gain,
+        query_weight, key_value_weight, out_weight,
     )
     return result.reshape(nlq, dlen, piece)
 

time: 108 us -> 91.2 us (0.84)
  the two profiles are of different devices: /device:TPU:11 before, /device:TPU:0 now
where the time goes in v2:
time: 91.2 us; the launch traced here: 91 us
  Pallas kernels  89.3 us (98%)
  local copies, waits for them, and re-layouts  1.67 us (2%)
    pallas_call x1, Pallas kernels, body(): pl.pallas_call(functools.partial(kernel, cfg), out_shape=jax.ShapeDtypeSt...  89.3 us

profile of v2, /device:TPU:0, one launch (start us, length us, event | category | flops | bytes accessed | tf_op | source)
XLA Modules:
  0.0 91.0 jit_solution(5504013119977543398)
XLA Ops:
  0.0 89.3 %reader.1 = bf16[128,1024]{1,0:T(8,128)(2,1)} custom-call(s32[4,4]{1,0:T(4,128)} %bitcast.7, bf16[128,4096]{1,0:T(8,128)(2,1)} %bitcast.5, bf16[4096]{0:T(1024)(128)(2,1)} %enc_gain.1, bf16[128,4096]{1,0:T(8,128)(2,1)} %bitcast.6, bf16[4096]{0:T(1024)(128)(2,1)} %dec_gain.1, bf16[4096,1024]{1,0:T(8,128)(2,1)} %qw.1, bf16[4096,2,1024]{2,1,0:T(2,128)(2,1)} %kvw.1, ...), custom_call_target="tpu_custom_call" | custom-call | tf_op jit(solution)/shard_map/reader/pallas_call | solution.py:395
  89.3 1.7 %copy.10 = bf16[2,64,1024]{2,1,0:T(8,128)(2,1)} copy(bf16[2,64,1024]{2,1,0:T(8,128)(2,1)} %bitcast.4) | data formatting | bytes 524288
